TPU v7x, 256 devices: a whole 4x4x8 slice. The times are simulated.
256 devices in a mesh: orb: 64 (over y, z, core), clu: 4 (over x).
Axes of the slice: x: 4, y: 4, z: 8, core: 2. Of those that a mesh axis runs over, the one named last changes fastest.
Arguments:
- integrals: bfloat16 [1024, 1024, 512], P('orb', 'clu'), may hold values from -1.1953125 to 1.1953125
- metric: bfloat16 [1024, 1024], P(None, 'orb'), may hold values from -0.1875 to 0.1875
- occ_energy: float32 [1024], replicated, may hold values from -2 to -0.5
- virt_energy: float32 [512], replicated, may hold values from 0.5 to 4
- orbital_order: int32 [4, 256], replicated, may hold values from 0 to 255, each once within a row
- pair_first: int32 [4, 64, 4], P('clu', 'orb'), may hold values from 0 to 3
- pair_second: int32 [4, 64, 4], replicated, may hold values from 0 to 255
- pair_live: int32 [4, 64, 4], P('clu', 'orb'), may hold values 0 or 1
Outputs:
- gamma: bfloat16 [1024, 1024, 512], P('orb', 'clu')
Inputs may be any that keep to these rules, and one draw needn't show every extreme that they name: `orbital_order`: each row is a permutation of 0 to 255. `pair_second`: slot s names an orbital of cluster s.
All inputs are finite; a program needn't handle non-finite values. No bound on the sum of `pair_live` on one device may be relied on, other than what follows from the above.
Results may differ from a plain program's by a relative error of at most 0.0052.
Values may be sent and summed in bfloat16 or wider, within the bound.
No kernel may reach another device: no remote copies, remote signals or barrier semaphores. Data moves between devices by JAX's collectives and lax.ppermute only.
A program may use at most 128 MiB of HBM per device.

v0:
```python
import functools

import jax
import jax.numpy as jnp
from jax import lax
from jax.experimental import pallas as pl
from jax.experimental.pallas import tpu as pltpu
from jax.sharding import PartitionSpec as P


LANES = 128
NZ, NC = 8, 2


def chosen(clu, rows):
    row = rows[0]
    for i in range(1, len(rows)):
        row = jnp.where(clu == i, rows[i], row)
    return row


def one_hot(row, count):
    lines = lax.broadcasted_iota(jnp.int32, (count, row.shape[1]), 0)
    return (lines == row).astype(jnp.float32)


def pick_kernel(clu_ref, index_ref, raw_ref, out_ref, turned, *, second):
    clu = clu_ref[0]
    xs, occ, width = raw_ref.shape
    if second:
        parts = [
            one_hot(chosen(clu, [index_ref[c, pl.ds(s, 1), :] for s in range(index_ref.shape[1])]), occ).T
            for c in range(index_ref.shape[0])
        ]
        picks = jnp.concatenate(parts, axis=0)
    else:
        picks = one_hot(chosen(clu, [index_ref[pl.ds(c, 1), :] for c in range(index_ref.shape[0])]), occ).T
    picks = picks.astype(jnp.bfloat16)
    count = picks.shape[0]
    for x in range(xs):
        rows = jnp.dot(picks, raw_ref[x], preferred_element_type=jnp.float32)
        for j in range(width // LANES):
            turned[j, pl.ds(x, count, stride=xs), :] = rows[:, j * LANES : (j + 1) * LANES]
    for j in range(width // LANES):
        out_ref[:, j * LANES : (j + 1) * LANES] = turned[j].astype(jnp.bfloat16)


def pick(clu, index, raw, count, second):
    xs, occ, virt = raw.shape
    block = 2 * LANES
    return pl.pallas_call(
        functools.partial(pick_kernel, second=second),
        grid=(virt // block,),
        in_specs=[
            pl.BlockSpec(memory_space=pltpu.SMEM),
            pl.BlockSpec(index.shape, lambda v: (0,) * index.ndim),
            pl.BlockSpec((xs, occ, block), lambda v: (0, 0, v)),
        ],
        out_specs=pl.BlockSpec((count * xs, block), lambda v: (0, v)),
        out_shape=jax.ShapeDtypeStruct((count * xs, virt), jnp.bfloat16),
        scratch_shapes=[pltpu.VMEM((block // LANES, count * xs, LANES), jnp.float32)],
        cost_estimate=pl.CostEstimate(
            flops=2 * xs * count * occ * virt, bytes_accessed=2 * xs * (count + occ) * virt, transcendentals=0
        ),
        name="pick_second" if second else "pick_owned",
    )(clu, index, raw)


def place_kernel(clu_ref, order_ref, back_ref, out_ref, turned):
    clu = clu_ref[0]
    xs, occ, width = out_ref.shape
    spots = one_hot(
        chosen(clu, [order_ref[pl.ds(c, 1), :] for c in range(order_ref.shape[0])]), occ
    ).astype(jnp.bfloat16)
    for j in range(width // LANES):
        turned[j] = back_ref[:, j * LANES : (j + 1) * LANES].astype(jnp.float32)
    for x in range(xs):
        rows = jnp.concatenate(
            [turned[j, pl.ds(x, occ, stride=xs), :] for j in range(width // LANES)], axis=1
        ).astype(jnp.bfloat16)
        out_ref[x] = jnp.dot(spots, rows, preferred_element_type=jnp.float32).astype(jnp.bfloat16)


def place(clu, order, back, xs):
    occ = order.shape[1]
    virt = back.shape[1]
    block = 2 * LANES
    return pl.pallas_call(
        place_kernel,
        grid=(virt // block,),
        in_specs=[
            pl.BlockSpec(memory_space=pltpu.SMEM),
            pl.BlockSpec(order.shape, lambda v: (0, 0)),
            pl.BlockSpec((occ * xs, block), lambda v: (0, v)),
        ],
        out_specs=pl.BlockSpec((xs, occ, block), lambda v: (0, 0, v)),
        out_shape=jax.ShapeDtypeStruct((xs, occ, virt), jnp.bfloat16),
        scratch_shapes=[pltpu.VMEM((block // LANES, occ * xs, LANES), jnp.float32)],
        cost_estimate=pl.CostEstimate(
            flops=2 * xs * occ * occ * virt, bytes_accessed=4 * xs * occ * virt, transcendentals=0
        ),
        name="place",
    )(clu, order, back)


def gamma_kernel(
    first_ref, scale_ref, own_ref, weight_ref, fit_ref, virt_row_ref, virt_col_ref, out_ref, total
):
    slot = pl.program_id(0)
    sources, _, xs, virt = own_ref.shape
    first = first_ref[slot]

    @pl.when(slot == 0)
    def _():
        total[...] = jnp.zeros(total.shape, total.dtype)

    raw = own_ref[:, 0].reshape(sources * xs, virt)
    crossed = jnp.dot(weight_ref[0], raw, preferred_element_type=jnp.float32)
    below = virt_col_ref[...] + virt_row_ref[...] - scale_ref[0, slot] - scale_ref[1, slot]
    amplitude = (scale_ref[2, slot] * crossed / below).astype(jnp.bfloat16)
    total[first] += jnp.dot(fit_ref[0], amplitude, preferred_element_type=jnp.float32)

    @pl.when(slot == pl.num_programs(0) - 1)
    def _():
        for k in range(out_ref.shape[1]):
            out_ref[:, k] = total[k].astype(jnp.bfloat16).reshape(sources, xs, virt)


def gamma_of(first, scale, own, weight, fit, virt_energy):
    sources, owned, xs, virt = own.shape
    slots, _, full = weight.shape
    return pl.pallas_call(
        gamma_kernel,
        grid_spec=pltpu.PrefetchScalarGridSpec(
            num_scalar_prefetch=2,
            grid=(slots,),
            in_specs=[
                pl.BlockSpec((sources, 1, xs, virt), lambda s, first, scale: (0, first[s], 0, 0)),
                pl.BlockSpec((1, virt, full), lambda s, first, scale: (s, 0, 0)),
                pl.BlockSpec((1, full, virt), lambda s, first, scale: (s, 0, 0)),
                pl.BlockSpec((1, virt), lambda s, first, scale: (0, 0)),
                pl.BlockSpec((virt, 1), lambda s, first, scale: (0, 0)),
            ],
            out_specs=pl.BlockSpec((sources, owned, xs, virt), lambda s, first, scale: (0, 0, 0, 0)),
            scratch_shapes=[pltpu.VMEM((owned, full, virt), jnp.float32)],
        ),
        out_shape=jax.ShapeDtypeStruct(own.shape, jnp.bfloat16),
        cost_estimate=pl.CostEstimate(
            flops=4 * slots * full * virt * virt, bytes_accessed=16 * full * virt * 2, transcendentals=0
        ),
        compiler_params=pltpu.CompilerParams(vmem_limit_bytes=48 * 1024 * 1024),
        name="gamma",
    )(first, scale, own, weight, fit, virt_energy[None, :], virt_energy[:, None])


def whole_metric(metric):
    orb_count = lax.axis_size("orb")
    ny = orb_count // (NZ * NC)
    half = NZ // 2
    here = lax.axis_index("orb")
    here_y, here_h, here_l, here_c = here // (NZ * NC), here // (2 * NC) % half, here // NC % 2, here % NC

    def send(block, to):
        pairs = []
        for y in range(ny):
            for h in range(half):
                for l in range(2):
                    for c in range(NC):
                        y2, h2, l2, c2 = to(y, h, l, c)
                        pairs.append(
                            (((y * half + h) * 2 + l) * NC + c, ((y2 * half + h2) * 2 + l2) * NC + c2)
                        )
        return lax.ppermute(block, "orb", pairs)

    def both(mine, other, here):
        return jnp.stack([jnp.where(here == 0, mine, other), jnp.where(here == 0, other, mine)])

    block = metric.T
    q, p = block.shape
    got = [send(block, lambda y, h, l, c, r=r: (y, (h + r) % half, l, c)) for r in range(1, half)]
    column = jnp.stack([block] + got)
    other = send(column, lambda y, h, l, c: (y, h, 1 - l, c))
    column = both(column, other, here_l)
    got = [send(column, lambda y, h, l, c, t=t: ((y + t) % ny, h, l, c)) for t in range(1, ny)]
    plane = jnp.stack([column] + got)
    other = send(plane, lambda y, h, l, c: (y, h, l, 1 - c))
    every = jnp.stack([plane, other]).reshape(orb_count, q, p)
    place = jnp.arange(orb_count, dtype=jnp.int32)
    y, h, l, c = place // (NZ * NC), place // (2 * NC) % half, place // NC % 2, place % NC
    spot = (((c + here_c) % NC * ny + (here_y - y) % ny) * 2 + l) * half + (here_h - h) % half
    return jnp.take(every, spot, axis=0, mode="clip").reshape(orb_count * q, p)


def window(
    integrals, metric, occ_energy, virt_energy, orbital_order, pair_first, pair_second, pair_live
):
    orb_count = lax.axis_size("orb")
    here_orb = lax.axis_index("orb")
    here_clu = lax.axis_index("clu")
    xs_rows, occ_count, virt = integrals.shape
    full_aux = metric.shape[0]
    owned = occ_count // orb_count
    slots = pair_second.shape[2]
    clu = here_clu.astype(jnp.int32)[None]

    wanted = pick(clu, pair_second.transpose(0, 2, 1), integrals, occ_count, True)
    seconds = lax.all_to_all(
        wanted.reshape(-1, xs_rows, virt), ("clu", "orb"), split_axis=0, concat_axis=0, tiled=True
    ).reshape(slots, full_aux, virt)

    mine = pick(clu, orbital_order, integrals, occ_count, False)
    own = lax.all_to_all(mine.reshape(orb_count, owned, xs_rows, virt), "orb", split_axis=0, concat_axis=0, tiled=True)

    turned = whole_metric(metric)
    fit = jnp.einsum("qp,spb->sqb", turned, seconds, preferred_element_type=jnp.float32).astype(jnp.bfloat16)
    weight = jnp.einsum("sqb,qp->sbp", fit, turned, preferred_element_type=jnp.float32).astype(jnp.bfloat16)

    first_slot = pair_first[0, 0]
    order = lax.dynamic_index_in_dim(orbital_order, here_clu, 0, keepdims=False)
    owned_orbs = lax.dynamic_slice_in_dim(order, here_orb * owned, owned) + here_clu * occ_count
    first_orb = jnp.take(owned_orbs, first_slot)
    own_second = lax.dynamic_slice(pair_second, (here_clu, here_orb, 0), (1, 1, slots))[0, 0]
    second_orb = own_second + jnp.arange(slots, dtype=jnp.int32) * occ_count
    scale = jnp.stack(
        [occ_energy[first_orb], occ_energy[second_orb], pair_live[0, 0].astype(jnp.float32)]
    )

    local = gamma_of(first_slot, scale, own, weight, fit, virt_energy)
    back = lax.all_to_all(local, "orb", split_axis=0, concat_axis=0, tiled=True)
    return place(clu, orbital_order, back.reshape(occ_count * xs_rows, virt), xs_rows)


def solution(mesh):
    in_specs = (
        P("orb", "clu", None),
        P(None, "orb"),
        P(),
        P(),
        P(),
        P("clu", "orb", None),
        P(),
        P("clu", "orb", None),
    )
    out_specs = P("orb", "clu", None)
    return jax.shard_map(window, mesh=mesh, in_specs=in_specs, out_specs=out_specs, check_vma=False)
```

profile of v0, /device:TPU:1, one launch (start us, length us, event | category | flops | bytes accessed | tf_op | source)
XLA Modules:
  0.0 385.7 jit_solution(10184383855675259357)
XLA Ops:
  0.0 0.0 copy-start
  0.0 7.0 %pick_second.1 = bf16[4096,512]{1,0:T(8,128)(2,1)} custom-call(s32[1]{0:T(128)} %bitcast.clu_ref, s32[4,4,64]{2,1,0:T(4,128)} %bitcast.88, bf16[16,256,512]{2,1,0:T(8,128)(2,1)} %raw_ref.3), custom_call_target="tpu_custom_call" | custom-call | flops 1073741824 | bytes 8388608 | tf_op jit(solution)/shard_map/pick_second/pallas_call | solution.py:51
  7.1 16.6 %all-to-all-start.1 = ((bf16[256,16,512]{2,1,0:T(8,128)(2,1)}), bf16[256,16,512]{2,1,0:T(8,128)(2,1)}, u32[]{:S(2)}, u32[]{:S(2)}) async-start(bf16[256,16,512]{2,1,0:T(8,128)(2,1)} %bitcast.68), calls=%async_computation.1 | async-start | bytes 8388608 | tf_op jit(solution)/shard_map/all_to_all | solution.py:207
  23.7 6.9 %pick_owned.1 = bf16[4096,512]{1,0:T(8,128)(2,1)} custom-call(s32[1]{0:T(128)} %bitcast.clu_ref, s32[4,256]{1,0:T(4,128)} %order_ref.1, bf16[16,256,512]{2,1,0:T(8,128)(2,1)} %raw_ref.3), custom_call_target="tpu_custom_call" | custom-call | flops 1073741824 | bytes 8388608 | tf_op jit(solution)/shard_map/pick_owned/pallas_call | solution.py:51
  30.6 91.9 %all-to-all-done.1 = bf16[256,16,512]{2,1,0:T(8,128)(2,1)} async-done(((bf16[256,16,512]{2,1,0:T(8,128)(2,1)}), bf16[256,16,512]{2,1,0:T(8,128)(2,1)}, u32[]{:S(2)}, u32[]{:S(2)}) %all-to-all-start.1) | async-done | bytes 4194336 | tf_op jit(solution)/shard_map/all_to_all | solution.py:207
  122.5 0.0 copy-start.5
  122.5 0.0 copy-start.2
  122.5 5.4 %all-to-all-start = ((bf16[64,4,16,512]{3,2,1,0:T(8,128)(2,1)}), bf16[64,4,16,512]{3,2,1,0:T(8,128)(2,1)}, u32[]{:S(2)}, u32[]{:S(2)}) async-start(bf16[64,4,16,512]{3,2,1,0:T(8,128)(2,1)} %bitcast.69), calls=%async_computation | async-start | bytes 8388608 | tf_op jit(solution)/shard_map/all_to_all | solution.py:212
  127.9 0.0 copy-start.1
  127.9 0.0 copy-start.6
  127.9 0.0 copy-done.5
  127.9 1.1 collective-permute-start
  129.0 3.3 collective-permute-start.1
  132.3 3.3 collective-permute-start.2
  135.6 86.1 %collective-permute-done = bf16[16,1024]{1,0:T(8,128)(2,1)S(1)} collective-permute-done((bf16[16,1024]{1,0:T(8,128)(2,1)S(1)}, bf16[16,1024]{1,0:T(8,128)(2,1)S(1)}, u32[]{:S(2)}, u32[]{:S(2)}) %collective-permute-start) | collective-permute-done | bytes 32800 | tf_op jit(solution)/shard_map/ppermute | solution.py:173
  221.7 3.4 collective-permute-done.1
  225.1 0.0 collective-permute-done.2
  225.1 0.1 collective-permute-start.3
  225.2 4.6 %collective-permute-done.3 = bf16[4,16,1024]{2,1,0:T(8,128)(2,1)S(1)} collective-permute-done((bf16[4,16,1024]{2,1,0:T(8,128)(2,1)S(1)}, bf16[4,16,1024]{2,1,0:T(8,128)(2,1)S(1)}, u32[]{:S(2)}, u32[]{:S(2)}) %collective-permute-start.3) | collective-permute-done | bytes 131104 | tf_op jit(solution)/shard_map/ppermute | solution.py:173
  229.9 0.1 collective-permute-start.4
  230.0 2.0 collective-permute-start.5
  231.9 1.1 collective-permute-start.6
  233.0 0.0 copy-done.2
  233.0 0.8 add_bitcast_fusion
  233.8 0.6 gather_fusion
  234.4 5.0 %collective-permute-done.4 = bf16[2,4,16,1024]{3,2,1,0:T(8,128)(2,1)S(1)} collective-permute-done((bf16[2,4,16,1024]{3,2,1,0:T(8,128)(2,1)S(1)}, bf16[2,4,16,1024]{3,2,1,0:T(8,128)(2,1)S(1)}, u32[]{:S(2)}, u32[]{:S(2)}) %collective-permute-start.4) | collective-permute-done | bytes 262176 | tf_op jit(solution)/shard_map/ppermute | solution.py:173
  239.4 1.9 collective-permute-done.5
  241.3 3.2 collective-permute-done.6
  244.6 0.2 fusion.19
  244.7 1.8 collective-permute-start.7
  246.6 0.9 dynamic-slice_reduce_fusion
  247.4 0.0 copy-done
  247.4 0.6 gather_fusion.1
  248.1 0.6 gather_fusion.2
  248.7 0.0 copy-done.1
  248.7 0.1 copy.14.virt_col_ref
  248.9 0.0 copy-done.6
  249.0 0.0 collective-permute-done.7
  249.0 1.4 pad_maximum_fusion
  250.4 2.1 gather_fusion.3
  252.5 0.0 copy-start.4
  252.5 7.5 %convert_bitcast_fusion.fit_ref = bf16[4,1024,512]{2,1,0:T(8,128)(2,1)S(1)} fusion(bf16[1024,1024,1]{1,0,2:T(8,128)(2,1)} %bitcast.72, bf16[4,1024,512]{2,1,0:T(8,128)(2,1)} %bitcast.14), kind=kOutput, calls=%fused_computation.4 | convolution fusion | flops 4297064448 | bytes 10485760 | tf_op jit(solution)/shard_map/qp,spb->sqb/dot_general | solution.py:215
  259.9 0.0 copy-start.3
  260.0 2.0 copy-done.3
  261.9 0.0 copy-done.4
  261.9 6.2 %convolution_convert_fusion.weight_ref = bf16[4,512,1024]{2,1,0:T(8,128)(2,1)} fusion(bf16[4,1024,512]{2,1,0:T(8,128)(2,1)S(1)} %convert_bitcast_fusion.fit_ref, bf16[1024,1024,1]{1,0,2:T(8,128)(2,1)S(1)} %bitcast.73), kind=kOutput, calls=%fused_computation.5 | convolution fusion | flops 4297064448 | bytes 10485760 | tf_op jit(solution)/shard_map/sqb,qp->sbp/dot_general | solution.py:216
  268.1 0.0 all-to-all-done.own_ref
  268.1 9.3 %gamma.1 = bf16[64,4,16,512]{3,2,1,0:T(8,128)(2,1)S(1)} custom-call(s32[4]{0:T(128)S(1)} %bitcast.67, f32[3,4]{1,0:T(4,128)S(1)} %pad_maximum_fusion.4.scale_ref, bf16[64,4,16,512]{3,2,1,0:T(8,128)(2,1)} %all-to-all-done.own_ref, bf16[4,512,1024]{2,1,0:T(8,128)(2,1)} %convolution_convert_fusion.weight_ref, bf16[4,1024,512]{2,1,0:T(8,128)(2,1)} %copy-done.3, ...), custom_call_target="tpu_custom_call" | custom-call | flops 4294967296 | bytes 16777216 | tf_op jit(solution)/shard_map/gamma/pallas_call | solution.py:132
  277.4 101.7 %all_to_all.15 = bf16[64,4,16,512]{3,2,1,0:T(8,128)(2,1)} all-to-all(bf16[64,4,16,512]{3,2,1,0:T(8,128)(2,1)S(1)} %gamma.1), channel_id=1, replica_groups=mesh['orb'=64,'clu'=4] {'orb'}, dimensions={0} | all-to-all | bytes 8388608 | tf_op jit(solution)/shard_map/all_to_all | solution.py:229
  379.1 6.6 %place.1 = bf16[16,256,512]{2,1,0:T(8,128)(2,1)} custom-call(s32[1]{0:T(128)} %bitcast.clu_ref, s32[4,256]{1,0:T(4,128)} %order_ref.1, bf16[4096,512]{1,0:T(8,128)(2,1)} %bitcast.70), custom_call_target="tpu_custom_call" | custom-call | flops 1073741824 | bytes 8388608 | tf_op jit(solution)/shard_map/place/pallas_call | solution.py:88
  (13 shorter events, 0.2 us)
Async XLA Ops:
  0.0 247.4 %copy-start = (f32[1024]{0:T(1024)S(1)}, f32[1024]{0:T(1024)}, u32[]{:S(2)}) copy-start(f32[1024]{0:T(1024)} %param.10) | copy-start | bytes 12292
  7.1 115.5 %all-to-all-start.1 = ((bf16[256,16,512]{2,1,0:T(8,128)(2,1)}), bf16[256,16,512]{2,1,0:T(8,128)(2,1)}, u32[]{:S(2)}, u32[]{:S(2)}) async-start(bf16[256,16,512]{2,1,0:T(8,128)(2,1)} %bitcast.68), calls=%async_computation.1 | async-start | bytes 8388608 | tf_op jit(solution)/shard_map/all_to_all | solution.py:207
  122.5 5.4 %copy-start.5 = (bf16[1024,16]{0,1:T(8,128)(2,1)S(1)}, bf16[1024,16]{0,1:T(8,128)(2,1)}, u32[]{:S(2)}) copy-start(bf16[1024,16]{0,1:T(8,128)(2,1)} %param.9) | copy-start | bytes 98308
  122.5 110.5 %copy-start.2 = (s32[1,1,4]{2,1,0:T(1,128)S(1)}, s32[1,1,4]{2,1,0:T(1,128)}, u32[]{:S(2)}) copy-start(s32[1,1,4]{2,1,0:T(1,128)} %param.13) | copy-start | bytes 52
  122.5 145.6 %all-to-all-start = ((bf16[64,4,16,512]{3,2,1,0:T(8,128)(2,1)}), bf16[64,4,16,512]{3,2,1,0:T(8,128)(2,1)}, u32[]{:S(2)}, u32[]{:S(2)}) async-start(bf16[64,4,16,512]{3,2,1,0:T(8,128)(2,1)} %bitcast.69), calls=%async_computation | async-start | bytes 8388608 | tf_op jit(solution)/shard_map/all_to_all | solution.py:212
  127.9 120.8 %copy-start.1 = (f32[512]{0:T(512)S(1)}, f32[512]{0:T(512)}, u32[]{:S(2)}) copy-start(f32[512]{0:T(512)} %param.11) | copy-start | bytes 6148
  127.9 121.0 %copy-start.6 = (s32[1,1,4]{2,1,0:T(1,128)S(1)}, s32[1,1,4]{2,1,0:T(1,128)}, u32[]{:S(2)}) copy-start(s32[1,1,4]{2,1,0:T(1,128)} %param.15) | copy-start | bytes 52
  127.9 93.8 %collective-permute-start = (bf16[16,1024]{1,0:T(8,128)(2,1)S(1)}, bf16[16,1024]{1,0:T(8,128)(2,1)S(1)}, u32[]{:S(2)}, u32[]{:S(2)}) collective-permute-start(bf16[16,1024]{1,0:T(8,128)(2,1)S(1)} %bitcast.77), channel_id=1, source_target_pairs={{0,16},{4,20},{8,24},{12,28},{16,32},{20,36},{24,40},{28,44},{32,4... | collective-permute-start | bytes 98312 | tf_op jit(solution)/shard_map/ppermute | solution.py:173
  129.0 96.1 %collective-permute-start.1 = (bf16[16,1024]{1,0:T(8,128)(2,1)S(1)}, bf16[16,1024]{1,0:T(8,128)(2,1)S(1)}, u32[]{:S(2)}, u32[]{:S(2)}) collective-permute-start(bf16[16,1024]{1,0:T(8,128)(2,1)S(1)} %bitcast.78), channel_id=1, source_target_pairs={{0,32},{4,36},{8,40},{12,44},{16,48},{20,52},{24,56},{28,60},{32,0... | collective-permute-start | bytes 98312 | tf_op jit(solution)/shard_map/ppermute | solution.py:173
  132.3 92.8 %collective-permute-start.2 = (bf16[16,1024]{1,0:T(8,128)(2,1)S(1)}, bf16[16,1024]{1,0:T(8,128)(2,1)S(1)}, u32[]{:S(2)}, u32[]{:S(2)}) collective-permute-start(bf16[16,1024]{1,0:T(8,128)(2,1)S(1)} %bitcast.79), channel_id=1, source_target_pairs={{0,48},{4,52},{8,56},{12,60},{16,0},{20,4},{24,8},{28,12},{32,16},... | collective-permute-start | bytes 98312 | tf_op jit(solution)/shard_map/ppermute | solution.py:173
  225.1 4.7 %collective-permute-start.3 = (bf16[4,16,1024]{2,1,0:T(8,128)(2,1)S(1)}, bf16[4,16,1024]{2,1,0:T(8,128)(2,1)S(1)}, u32[]{:S(2)}, u32[]{:S(2)}) collective-permute-start(bf16[4,16,1024]{2,1,0:T(8,128)(2,1)S(1)} %pad_maximum_fusion.3), channel_id=1, source_target_pairs={{0,8},{4,12},{8,0},{12,4},{16,24},{20,28},{24,16},{28,20},{32,40},... | collective-permute-start | bytes 393224 | tf_op jit(solution)/shard_map/ppermute | solution.py:173
  229.9 9.6 %collective-permute-start.4 = (bf16[2,4,16,1024]{3,2,1,0:T(8,128)(2,1)S(1)}, bf16[2,4,16,1024]{3,2,1,0:T(8,128)(2,1)S(1)}, u32[]{:S(2)}, u32[]{:S(2)}) collective-permute-start(bf16[2,4,16,1024]{3,2,1,0:T(8,128)(2,1)S(1)} %get-tuple-element.8), channel_id=1, source_target_pairs={{0,64},{4,68},{8,72},{12,76},{16,80},{20,84},{24,88},{28,92},{32,9... | collective-permute-start | bytes 786440 | tf_op jit(solution)/shard_map/ppermute | solution.py:173
  230.0 11.4 %collective-permute-start.5 = (bf16[2,4,16,1024]{3,2,1,0:T(8,128)(2,1)S(1)}, bf16[2,4,16,1024]{3,2,1,0:T(8,128)(2,1)S(1)}, u32[]{:S(2)}, u32[]{:S(2)}) collective-permute-start(bf16[2,4,16,1024]{3,2,1,0:T(8,128)(2,1)S(1)} %get-tuple-element.8), channel_id=1, source_target_pairs={{0,128},{4,132},{8,136},{12,140},{16,144},{20,148},{24,152},{28,15... | collective-permute-start | bytes 786440 | tf_op jit(solution)/shard_map/ppermute | solution.py:173
  231.9 12.6 %collective-permute-start.6 = (bf16[2,4,16,1024]{3,2,1,0:T(8,128)(2,1)S(1)}, bf16[2,4,16,1024]{3,2,1,0:T(8,128)(2,1)S(1)}, u32[]{:S(2)}, u32[]{:S(2)}) collective-permute-start(bf16[2,4,16,1024]{3,2,1,0:T(8,128)(2,1)S(1)} %get-tuple-element.8), channel_id=1, source_target_pairs={{0,192},{4,196},{8,200},{12,204},{16,208},{20,212},{24,216},{28,22... | collective-permute-start | bytes 786440 | tf_op jit(solution)/shard_map/ppermute | solution.py:173
  244.7 4.2 %collective-permute-start.7 = (bf16[4,2,4,16,1024]{4,3,2,1,0:T(8,128)(2,1)S(1)}, bf16[4,2,4,16,1024]{4,3,2,1,0:T(8,128)(2,1)}, u32[]{:S(2)}, u32[]{:S(2)}) collective-permute-start(bf16[4,2,4,16,1024]{4,3,2,1,0:T(8,128)(2,1)S(1)} %get-tuple-element.6), channel_id=1, source_target_pairs={{0,4},{4,0},{8,12},{12,8},{16,20},{20,16},{24,28},{28,24},{32,36},... | collective-permute-start | bytes 3145736 | tf_op jit(solution)/shard_map/ppermute | solution.py:173
  252.5 9.5 %copy-start.4 = (bf16[64,16,1024]{2,1,0:T(8,128)(2,1)S(1)}, bf16[64,16,1024]{2,1,0:T(8,128)(2,1)}, u32[]{:S(2)}) copy-start(bf16[64,16,1024]{2,1,0:T(8,128)(2,1)} %gather_fusion.3) | copy-start | bytes 6291460
  259.9 2.0 copy-start.3
where the time goes:
time: 386 us
  waiting for transfers between devices  196 us (51%)
  blocking collectives  102 us (26%)
  starting transfers between devices  34.7 us (9%)
  Pallas kernels  29.8 us (8%)
  matrix products  13.6 us (4%)
  local copies, waits for them, and re-layouts  6.98 us (2%)
    ppermute x8, waiting for transfers between devices, send(): return lax.ppermute(block, 'orb', pairs)  104 us
    all_to_all x1, blocking collectives, window(): back = lax.all_to_all(local, 'orb', split_axis=0, concat_axis=0, tiled=True)  102 us
    all_to_all x1, waiting for transfers between devices, window(): lax.all_to_all(wanted.reshape(-1, xs_rows, virt), ('clu', 'orb'), split_a...  91.9 us
    all_to_all x1, starting transfers between devices, window(): lax.all_to_all(wanted.reshape(-1, xs_rows, virt), ('clu', 'orb'), split_a...  16.6 us
    pallas_call x2, Pallas kernels, pick(): pl.pallas_call(functools.partial(pick_kernel, second=second), grid=(virt...  13.9 us
    ppermute x8, starting transfers between devices, send(): return lax.ppermute(block, 'orb', pairs)  12.7 us
    pallas_call x1, Pallas kernels, gamma_of(): pl.pallas_call(gamma_kernel, grid_spec=pltpu.PrefetchScalarGridSpec(num_s...  9.32 us
  transfers between devices with their start and end apart: 10, of which 7 were waited for; matrix products, arithmetic and copies ran while one was open for 5% of the time, Pallas kernels for 2%

commit v1 on v0

v1 whole, which is shorter than its diff:
```python
import functools

import jax
import jax.numpy as jnp
from jax import lax
from jax.experimental import pallas as pl
from jax.experimental.pallas import tpu as pltpu
from jax.sharding import PartitionSpec as P


BLOCK, GROUP = 256, 16
NZ, NC = 8, 2


def chosen(clu, rows):
    row = rows[0]
    for i in range(1, len(rows)):
        row = jnp.where(clu == i, rows[i], row)
    return row


def one_hot(row, count):
    lines = lax.broadcasted_iota(jnp.int32, (count, row.shape[1]), 0)
    return (lines == row).astype(jnp.float32)


def turning(rows, cols):
    count = rows * cols
    to = lax.broadcasted_iota(jnp.int32, (count, count), 0)
    at = lax.broadcasted_iota(jnp.int32, (count, count), 1)
    return ((at // cols == to % rows) & (at % cols == to // rows)).astype(jnp.float32).astype(jnp.bfloat16)


def pick_kernel(clu_ref, index_ref, raw_ref, out_ref, middle, *, second):
    clu = clu_ref[0]
    xs, occ, width = raw_ref.shape
    if second:
        parts = [
            one_hot(chosen(clu, [index_ref[c, pl.ds(s, 1), :] for s in range(index_ref.shape[1])]), occ).T
            for c in range(index_ref.shape[0])
        ]
        picks = jnp.concatenate(parts, axis=0)
    else:
        picks = one_hot(chosen(clu, [index_ref[pl.ds(c, 1), :] for c in range(index_ref.shape[0])]), occ).T
    picks = picks.astype(jnp.bfloat16)
    for x in range(xs):
        middle[x] = jnp.dot(picks, raw_ref[x], preferred_element_type=jnp.float32).astype(jnp.bfloat16)
    turn = turning(xs, GROUP)
    for g in range(picks.shape[0] // GROUP):
        lines = middle[:, g * GROUP : (g + 1) * GROUP, :].reshape(xs * GROUP, width)
        out_ref[g * GROUP * xs : (g + 1) * GROUP * xs, :] = jnp.dot(
            turn, lines, preferred_element_type=jnp.float32
        ).astype(jnp.bfloat16)


def pick(clu, index, raw, count, second):
    xs, occ, virt = raw.shape
    return pl.pallas_call(
        functools.partial(pick_kernel, second=second),
        grid=(virt // BLOCK,),
        in_specs=[
            pl.BlockSpec(memory_space=pltpu.SMEM),
            pl.BlockSpec(index.shape, lambda v: (0,) * index.ndim),
            pl.BlockSpec((xs, occ, BLOCK), lambda v: (0, 0, v)),
        ],
        out_specs=pl.BlockSpec((count * xs, BLOCK), lambda v: (0, v)),
        out_shape=jax.ShapeDtypeStruct((count * xs, virt), jnp.bfloat16),
        scratch_shapes=[pltpu.VMEM((xs, count, BLOCK), jnp.bfloat16)],
        cost_estimate=pl.CostEstimate(
            flops=4 * xs * count * occ * virt, bytes_accessed=2 * xs * (count + occ) * virt, transcendentals=0
        ),
        name="pick_second" if second else "pick_owned",
    )(clu, index, raw)


def place_kernel(clu_ref, order_ref, back_ref, out_ref, middle):
    clu = clu_ref[0]
    xs, occ, width = out_ref.shape
    spots = one_hot(
        chosen(clu, [order_ref[pl.ds(c, 1), :] for c in range(order_ref.shape[0])]), occ
    ).astype(jnp.bfloat16)
    turn = turning(GROUP, xs)
    for g in range(occ // GROUP):
        lines = back_ref[g * GROUP * xs : (g + 1) * GROUP * xs, :]
        middle[:, g * GROUP : (g + 1) * GROUP, :] = (
            jnp.dot(turn, lines, preferred_element_type=jnp.float32)
            .astype(jnp.bfloat16)
            .reshape(xs, GROUP, width)
        )
    for x in range(xs):
        out_ref[x] = jnp.dot(spots, middle[x], preferred_element_type=jnp.float32).astype(jnp.bfloat16)


def place(clu, order, back, xs):
    occ = order.shape[1]
    virt = back.shape[1]
    return pl.pallas_call(
        place_kernel,
        grid=(virt // BLOCK,),
        in_specs=[
            pl.BlockSpec(memory_space=pltpu.SMEM),
            pl.BlockSpec(order.shape, lambda v: (0, 0)),
            pl.BlockSpec((occ * xs, BLOCK), lambda v: (0, v)),
        ],
        out_specs=pl.BlockSpec((xs, occ, BLOCK), lambda v: (0, 0, v)),
        out_shape=jax.ShapeDtypeStruct((xs, occ, virt), jnp.bfloat16),
        scratch_shapes=[pltpu.VMEM((xs, occ, BLOCK), jnp.bfloat16)],
        cost_estimate=pl.CostEstimate(
            flops=4 * xs * occ * occ * virt, bytes_accessed=4 * xs * occ * virt, transcendentals=0
        ),
        name="place",
    )(clu, order, back)


def gamma_kernel(
    slot_ref, first_ref, scale_ref, virt_row_ref, virt_col_ref, own_hbm, weight_hbm, fit_hbm, out_hbm,
    own, weight, fit, amplitude, total, rounded, blank, own_in, weight_in, fit_in, sent, blanked,
):
    slots = weight.shape[0]
    owned = out_hbm.shape[1]
    full, virt = total.shape
    slot = [slot_ref[t] for t in range(slots)]
    first = [first_ref[t] for t in range(slots)]
    used = [functools.reduce(jnp.logical_or, [f == k for f in first]) for k in range(owned)]
    copy = pltpu.make_async_copy
    own_copy = [copy(own_hbm.at[:, first[t]], own.at[t], own_in.at[t]) for t in range(slots)]
    weight_copy = [copy(weight_hbm.at[slot[t]], weight.at[t], weight_in.at[t]) for t in range(slots)]
    fit_copy = [copy(fit_hbm.at[slot[t]], fit.at[t], fit_in.at[t]) for t in range(slots)]
    send = [copy(rounded.at[t], out_hbm.at[:, first[t]], sent.at[t]) for t in range(slots)]
    clear = [copy(blank, out_hbm.at[:, k], blanked.at[k]) for k in range(owned)]
    for t in range(slots):
        own_copy[t].start()
        weight_copy[t].start()
        fit_copy[t].start()
    blank[...] = jnp.zeros(blank.shape, blank.dtype)
    for k in range(owned):
        @pl.when(jnp.logical_not(used[k]))
        def _(k=k):
            clear[k].start()

    for t in range(slots):
        own_copy[t].wait()
        weight_copy[t].wait()
        crossed = jnp.dot(weight[t], own[t].reshape(full, virt), preferred_element_type=jnp.float32)
        below = virt_col_ref[...] + virt_row_ref[...] - scale_ref[0, slot[t]] - scale_ref[1, slot[t]]
        amplitude[...] = (crossed * (scale_ref[2, slot[t]] / below)).astype(jnp.bfloat16)
        fit_copy[t].wait()
        part = jnp.dot(fit[t], amplitude[...], preferred_element_type=jnp.float32)
        if t > 0:
            part = part + jnp.where(first[t] == first[t - 1], total[...], 0.0)
        if t < slots - 1:
            total[...] = part
        rounded[t] = part.astype(jnp.bfloat16).reshape(rounded.shape[1:])
        if t < slots - 1:
            @pl.when(first[t] != first[t + 1])
            def _(t=t):
                send[t].start()
        else:
            send[t].start()

    for t in range(slots - 1):
        @pl.when(first[t] != first[t + 1])
        def _(t=t):
            send[t].wait()

    send[slots - 1].wait()
    for k in range(owned):
        @pl.when(jnp.logical_not(used[k]))
        def _(k=k):
            clear[k].wait()


def gamma_of(first, scale, own, weight, fit, virt_energy):
    sources, owned, xs, virt = own.shape
    slots, _, full = weight.shape
    number = jnp.arange(slots, dtype=jnp.int32)
    key = first * slots + number
    rank = jnp.sum((key[:, None] > key[None, :]).astype(jnp.int32), axis=1)
    at = (rank[None, :] == number[:, None]).astype(jnp.int32)
    hbm = pl.BlockSpec(memory_space=pltpu.HBM)
    smem = pl.BlockSpec(memory_space=pltpu.SMEM)
    vmem = pl.BlockSpec(memory_space=pltpu.VMEM)
    dma = pltpu.SemaphoreType.DMA
    return pl.pallas_call(
        gamma_kernel,
        in_specs=[smem, smem, smem, vmem, vmem, hbm, hbm, hbm],
        out_specs=hbm,
        out_shape=jax.ShapeDtypeStruct(own.shape, jnp.bfloat16),
        scratch_shapes=[
            pltpu.VMEM((slots, sources, xs, virt), jnp.bfloat16),
            pltpu.VMEM((slots, virt, full), jnp.bfloat16),
            pltpu.VMEM((slots, full, virt), jnp.bfloat16),
            pltpu.VMEM((virt, virt), jnp.bfloat16),
            pltpu.VMEM((full, virt), jnp.float32),
            pltpu.VMEM((slots, sources, xs, virt), jnp.bfloat16),
            pltpu.VMEM((sources, xs, virt), jnp.bfloat16),
            dma((slots,)),
            dma((slots,)),
            dma((slots,)),
            dma((slots,)),
            dma((owned,)),
        ],
        cost_estimate=pl.CostEstimate(
            flops=4 * slots * full * virt * virt, bytes_accessed=16 * full * virt * 2, transcendentals=0
        ),
        compiler_params=pltpu.CompilerParams(vmem_limit_bytes=52 * 1024 * 1024),
        name="gamma",
    )(
        jnp.sum(at * number[None, :], axis=1),
        jnp.sum(at * first[None, :], axis=1),
        scale,
        virt_energy[None, :],
        virt_energy[:, None],
        own,
        weight,
        fit,
    )


def whole_metric(metric):
    orb_count = lax.axis_size("orb")
    ny = orb_count // (NZ * NC)
    here = lax.axis_index("orb")
    here_y, here_z, here_c = here // (NZ * NC), here // NC % NZ, here % NC
    spots = [(y, z, c) for y in range(ny) for z in range(NZ) for c in range(NC)]

    def send(block, dy, dz, dc):
        pairs = [
            (
                (y * NZ + z) * NC + c,
                ((y + dy) % ny * NZ + (z + dz) % NZ) * NC + (c + dc) % NC,
            )
            for y, z, c in spots
        ]
        return lax.ppermute(block, "orb", pairs)

    block = metric.T
    q, p = block.shape
    got = [send(block, 0, k, 0) for k in range(1, NZ)]
    column = jnp.stack([block] + got)
    got = [send(column, k, 0, 0) for k in range(1, ny)]
    plane = jnp.stack([column] + got)
    got = [send(plane, 0, 0, k) for k in range(1, NC)]
    every = jnp.stack([plane] + got).reshape(orb_count, q, p)
    place = jnp.arange(orb_count, dtype=jnp.int32)
    y, z, c = place // (NZ * NC), place // NC % NZ, place % NC
    spot = ((here_c - c) % NC * ny + (here_y - y) % ny) * NZ + (here_z - z) % NZ
    return jnp.take(every, spot, axis=0, mode="clip").reshape(orb_count * q, p)


def window(
    integrals, metric, occ_energy, virt_energy, orbital_order, pair_first, pair_second, pair_live
):
    orb_count = lax.axis_size("orb")
    here_orb = lax.axis_index("orb")
    here_clu = lax.axis_index("clu")
    xs_rows, occ_count, virt = integrals.shape
    full_aux = metric.shape[0]
    owned = occ_count // orb_count
    slots = pair_second.shape[2]
    clu = here_clu.astype(jnp.int32)[None]

    wanted = pick(clu, pair_second.transpose(0, 2, 1), integrals, occ_count, True)
    seconds = lax.all_to_all(
        wanted.reshape(-1, xs_rows, virt), ("clu", "orb"), split_axis=0, concat_axis=0, tiled=True
    ).reshape(slots, full_aux, virt)

    mine = pick(clu, orbital_order, integrals, occ_count, False)
    own = lax.all_to_all(mine.reshape(orb_count, owned, xs_rows, virt), "orb", split_axis=0, concat_axis=0, tiled=True)

    turned = whole_metric(metric)
    fit = jnp.einsum("qp,spb->sqb", turned, seconds, preferred_element_type=jnp.float32).astype(jnp.bfloat16)
    weight = jnp.einsum("sqb,qp->sbp", fit, turned, preferred_element_type=jnp.float32).astype(jnp.bfloat16)

    first_slot = pair_first[0, 0]
    order = lax.dynamic_index_in_dim(orbital_order, here_clu, 0, keepdims=False)
    owned_orbs = lax.dynamic_slice_in_dim(order, here_orb * owned, owned) + here_clu * occ_count
    first_orb = jnp.take(owned_orbs, first_slot)
    own_second = lax.dynamic_slice(pair_second, (here_clu, here_orb, 0), (1, 1, slots))[0, 0]
    second_orb = own_second + jnp.arange(slots, dtype=jnp.int32) * occ_count
    scale = jnp.stack(
        [occ_energy[first_orb], occ_energy[second_orb], pair_live[0, 0].astype(jnp.float32)]
    )

    local = gamma_of(first_slot, scale, own, weight, fit, virt_energy)
    back = lax.all_to_all(local, "orb", split_axis=0, concat_axis=0, tiled=True)
    return place(clu, orbital_order, back.reshape(occ_count * xs_rows, virt), xs_rows)


def solution(mesh):
    in_specs = (
        P("orb", "clu", None),
        P(None, "orb"),
        P(),
        P(),
        P(),
        P("clu", "orb", None),
        P(),
        P("clu", "orb", None),
    )
    out_specs = P("orb", "clu", None)
    return jax.shard_map(window, mesh=mesh, in_specs=in_specs, out_specs=out_specs, check_vma=False)
```

time: 386 us -> 384 us (level)
  waiting for transfers between devices: 196 us -> 189 us
  starting transfers between devices: 34.7 us -> 40.1 us
    ppermute x8 -> x11, waiting for transfers between devices: 104 us -> 96.3 us  [send(): return lax.ppermute(block, 'orb', pairs)]
    ppermute x8 -> x11, starting transfers between devices: 12.7 us -> 18.1 us  [send(): return lax.ppermute(block, 'orb', pairs)]
  transfers between devices with their start and end apart: 10 -> 13, of which waited for: 7 -> 8; matrix products, arithmetic and copies ran while one was open for 5% -> 6% of each run, Pallas kernels for 2% -> 2%
where the time goes in v1:
time: 384 us; the launch traced here: 383 us
  waiting for transfers between devices  189 us (49%)
  blocking collectives  102 us (27%)
  starting transfers between devices  40.1 us (10%)
  Pallas kernels  26.7 us (7%)
  matrix products  13.6 us (4%)
  local copies, waits for them, and re-layouts  8.04 us (2%)
    all_to_all x1, blocking collectives, window(): back = lax.all_to_all(local, 'orb', split_axis=0, concat_axis=0, tiled=True)  102 us
    ppermute x11, waiting for transfers between devices, send(): return lax.ppermute(block, 'orb', pairs)  96.3 us
    all_to_all x1, waiting for transfers between devices, window(): lax.all_to_all(wanted.reshape(-1, xs_rows, virt), ('clu', 'orb'), split_a...  93 us
    ppermute x11, starting transfers between devices, send(): return lax.ppermute(block, 'orb', pairs)  18.1 us
    all_to_all x1, starting transfers between devices, window(): lax.all_to_all(wanted.reshape(-1, xs_rows, virt), ('clu', 'orb'), split_a...  16.6 us
    pallas_call x2, Pallas kernels, pick(): pl.pallas_call(functools.partial(pick_kernel, second=second), grid=(virt...  11.6 us
    pallas_call x1, Pallas kernels, gamma_of(): pl.pallas_call(gamma_kernel, in_specs=[smem, smem, smem, vmem, vmem, hbm,...  9.51 us
  transfers between devices with their start and end apart: 13, of which 8 were waited for; matrix products, arithmetic and copies ran while one was open for 6% of the time, Pallas kernels for 2%

profile of v1, /device:TPU:1, one launch (start us, length us, event | category | flops | bytes accessed | tf_op | source)
XLA Modules:
  0.0 383.2 jit_solution(14050751909760336290)
XLA Ops:
  0.0 0.0 copy-start
  0.0 5.8 %pick_second.1 = bf16[4096,512]{1,0:T(8,128)(2,1)} custom-call(s32[1]{0:T(128)} %bitcast.clu_ref, s32[4,4,64]{2,1,0:T(4,128)} %bitcast.93, bf16[16,256,512]{2,1,0:T(8,128)(2,1)} %raw_ref.3), custom_call_target="tpu_custom_call" | custom-call | flops 2147483648 | bytes 8388608 | tf_op jit(solution)/shard_map/pick_second/pallas_call | solution.py:58
  5.8 16.6 %all-to-all-start.1 = ((bf16[256,16,512]{2,1,0:T(8,128)(2,1)}), bf16[256,16,512]{2,1,0:T(8,128)(2,1)}, u32[]{:S(2)}, u32[]{:S(2)}) async-start(bf16[256,16,512]{2,1,0:T(8,128)(2,1)} %bitcast.75), calls=%async_computation.1 | async-start | bytes 8388608 | tf_op jit(solution)/shard_map/all_to_all | solution.py:264
  22.5 5.8 %pick_owned.1 = bf16[4096,512]{1,0:T(8,128)(2,1)} custom-call(s32[1]{0:T(128)} %bitcast.clu_ref, s32[4,256]{1,0:T(4,128)} %order_ref.1, bf16[16,256,512]{2,1,0:T(8,128)(2,1)} %raw_ref.3), custom_call_target="tpu_custom_call" | custom-call | flops 2147483648 | bytes 8388608 | tf_op jit(solution)/shard_map/pick_owned/pallas_call | solution.py:58
  28.3 93.0 %all-to-all-done.1 = bf16[256,16,512]{2,1,0:T(8,128)(2,1)} async-done(((bf16[256,16,512]{2,1,0:T(8,128)(2,1)}), bf16[256,16,512]{2,1,0:T(8,128)(2,1)}, u32[]{:S(2)}, u32[]{:S(2)}) %all-to-all-start.1) | async-done | bytes 4194336 | tf_op jit(solution)/shard_map/all_to_all | solution.py:264
  121.3 0.0 copy-start.5
  121.3 0.0 copy-start.6
  121.3 5.4 %all-to-all-start = ((bf16[64,4,16,512]{3,2,1,0:T(8,128)(2,1)}), bf16[64,4,16,512]{3,2,1,0:T(8,128)(2,1)}, u32[]{:S(2)}, u32[]{:S(2)}) async-start(bf16[64,4,16,512]{3,2,1,0:T(8,128)(2,1)} %bitcast.76), calls=%async_computation | async-start | bytes 8388608 | tf_op jit(solution)/shard_map/all_to_all | solution.py:269
  126.7 0.0 copy-start.1
  126.7 0.0 copy-start.7
  126.7 0.0 copy-done.5
  126.7 0.9 collective-permute-start
  127.6 1.4 collective-permute-start.1
  129.0 2.4 collective-permute-start.2
  131.4 2.1 collective-permute-start.3
  133.4 2.4 collective-permute-start.4
  135.8 0.9 dynamic-slice_reduce_fusion
  136.7 0.0 copy-done.6
  136.8 80.3 %collective-permute-done = bf16[16,1024]{1,0:T(8,128)(2,1)S(1)} collective-permute-done((bf16[16,1024]{1,0:T(8,128)(2,1)S(1)}, bf16[16,1024]{1,0:T(8,128)(2,1)S(1)}, u32[]{:S(2)}, u32[]{:S(2)}) %collective-permute-start) | collective-permute-done | bytes 32800 | tf_op jit(solution)/shard_map/ppermute | solution.py:235
  217.1 1.7 collective-permute-start.5
  218.8 2.2 collective-permute-done.1
  221.0 1.7 collective-permute-start.6
  222.8 0.0 collective-permute-done.2
  222.8 3.8 collective-permute-done.3
  226.6 0.0 collective-permute-done.4
  226.6 0.0 collective-permute-done.5
  226.7 0.0 collective-permute-done.6
  226.7 0.2 collective-permute-start.7
  226.9 2.6 collective-permute-start.8
  229.5 1.1 collective-permute-start.9
  230.6 0.0 copy-done
  230.6 0.6 gather_fusion.2
  231.2 0.8 add_bitcast_fusion
  232.0 0.6 gather_fusion
  232.6 3.7 collective-permute-done.7
  236.3 3.2 collective-permute-done.8
  239.5 1.9 collective-permute-done.9
  241.4 0.2 fusion.15
  241.6 1.6 collective-permute-start.10
  243.2 0.6 gather_fusion.1
  243.8 0.0 copy-done.1
  243.8 0.1 copy.18.virt_col_ref
  244.0 0.0 copy-done.7
  244.0 0.2 convert_reduce_fusion
  244.2 0.1 select_reduce_fusion
  244.4 1.1 collective-permute-done.10
  245.5 0.0 copy-start.4
  245.5 1.1 copy-done.4
  246.6 1.4 pad_maximum_fusion
  248.0 2.1 gather_fusion.3
  250.0 0.0 copy-start.3
  250.0 7.5 %convert_bitcast_fusion.fit_hbm = bf16[4,1024,512]{2,1,0:T(8,128)(2,1)S(1)} fusion(bf16[1024,1024,1]{1,0,2:T(8,128)(2,1)} %bitcast.79, bf16[4,1024,512]{2,1,0:T(8,128)(2,1)} %bitcast.16), kind=kOutput, calls=%fused_computation.4 | convolution fusion | flops 4297064448 | bytes 10485760 | tf_op jit(solution)/shard_map/qp,spb->sqb/dot_general | solution.py:272
  257.5 0.0 copy-start.2
  257.5 2.0 copy-done.2
  259.5 0.0 copy-done.3
  259.5 6.1 %convolution_convert_fusion.weight_hbm = bf16[4,512,1024]{2,1,0:T(8,128)(2,1)} fusion(bf16[4,1024,512]{2,1,0:T(8,128)(2,1)S(1)} %convert_bitcast_fusion.fit_hbm, bf16[1024,1024,1]{1,0,2:T(8,128)(2,1)S(1)} %bitcast.80), kind=kOutput, calls=%fused_computation.5 | convolution fusion | flops 4297064448 | bytes 10485760 | tf_op jit(solution)/shard_map/sqb,qp->sbp/dot_general | solution.py:273
  265.6 0.0 all-to-all-done.own_hbm
  265.6 9.5 %gamma.1 = bf16[64,4,16,512]{3,2,1,0:T(8,128)(2,1)} custom-call(s32[4]{0:T(128)S(1)} %get-tuple-element.6.slot_ref, s32[4]{0:T(128)S(1)} %get-tuple-element.5.first_ref, f32[3,4]{1,0:T(4,128)S(1)} %pad_maximum_fusion.2.scale_ref, f32[1,512]{1,0:T(1,128)S(1)} %bitcast.74, f32[512,1]{1,0:T(8,128)S(1)} %copy.18.virt_col_ref, ...), custom_call_target="tpu_custom_call" | custom-call | flops 4294967296 | bytes 16777216 | tf_op jit(solution)/shard_map/gamma/pallas_call | solution.py:184
  275.1 102.4 %all_to_all.15 = bf16[64,4,16,512]{3,2,1,0:T(8,128)(2,1)} all-to-all(bf16[64,4,16,512]{3,2,1,0:T(8,128)(2,1)} %gamma.1), channel_id=1, replica_groups=mesh['orb'=64,'clu'=4] {'orb'}, dimensions={0} | all-to-all | bytes 8388608 | tf_op jit(solution)/shard_map/all_to_all | solution.py:286
  377.5 5.6 %place.1 = bf16[16,256,512]{2,1,0:T(8,128)(2,1)} custom-call(s32[1]{0:T(128)} %bitcast.clu_ref, s32[4,256]{1,0:T(4,128)} %order_ref.1, bf16[4096,512]{1,0:T(8,128)(2,1)} %bitcast.77), custom_call_target="tpu_custom_call" | custom-call | flops 2147483648 | bytes 8388608 | tf_op jit(solution)/shard_map/place/pallas_call | solution.py:97
  (18 shorter events, 0.1 us)
Async XLA Ops:
  0.0 230.6 %copy-start = (f32[1024]{0:T(1024)S(1)}, f32[1024]{0:T(1024)}, u32[]{:S(2)}) copy-start(f32[1024]{0:T(1024)} %param.10) | copy-start | bytes 12292
  5.8 115.5 %all-to-all-start.1 = ((bf16[256,16,512]{2,1,0:T(8,128)(2,1)}), bf16[256,16,512]{2,1,0:T(8,128)(2,1)}, u32[]{:S(2)}, u32[]{:S(2)}) async-start(bf16[256,16,512]{2,1,0:T(8,128)(2,1)} %bitcast.75), calls=%async_computation.1 | async-start | bytes 8388608 | tf_op jit(solution)/shard_map/all_to_all | solution.py:264
  121.3 5.4 %copy-start.5 = (bf16[1024,16]{0,1:T(8,128)(2,1)S(1)}, bf16[1024,16]{0,1:T(8,128)(2,1)}, u32[]{:S(2)}) copy-start(bf16[1024,16]{0,1:T(8,128)(2,1)} %param.9) | copy-start | bytes 98308
  121.3 15.4 %copy-start.6 = (s32[1,1,4]{2,1,0:T(1,128)S(1)}, s32[1,1,4]{2,1,0:T(1,128)}, u32[]{:S(2)}) copy-start(s32[1,1,4]{2,1,0:T(1,128)} %param.13) | copy-start | bytes 52
  121.3 144.3 %all-to-all-start = ((bf16[64,4,16,512]{3,2,1,0:T(8,128)(2,1)}), bf16[64,4,16,512]{3,2,1,0:T(8,128)(2,1)}, u32[]{:S(2)}, u32[]{:S(2)}) async-start(bf16[64,4,16,512]{3,2,1,0:T(8,128)(2,1)} %bitcast.76), calls=%async_computation | async-start | bytes 8388608 | tf_op jit(solution)/shard_map/all_to_all | solution.py:269
  126.7 117.1 %copy-start.1 = (f32[512]{0:T(512)S(1)}, f32[512]{0:T(512)}, u32[]{:S(2)}) copy-start(f32[512]{0:T(512)} %param.11) | copy-start | bytes 6148
  126.7 117.3 %copy-start.7 = (s32[1,1,4]{2,1,0:T(1,128)S(1)}, s32[1,1,4]{2,1,0:T(1,128)}, u32[]{:S(2)}) copy-start(s32[1,1,4]{2,1,0:T(1,128)} %param.15) | copy-start | bytes 52
  126.7 90.4 %collective-permute-start = (bf16[16,1024]{1,0:T(8,128)(2,1)S(1)}, bf16[16,1024]{1,0:T(8,128)(2,1)S(1)}, u32[]{:S(2)}, u32[]{:S(2)}) collective-permute-start(bf16[16,1024]{1,0:T(8,128)(2,1)S(1)} %bitcast.86), channel_id=1, source_target_pairs={{0,8},{4,12},{8,16},{12,20},{16,24},{20,28},{24,32},{28,36},{32,40... | collective-permute-start | bytes 98312 | tf_op jit(solution)/shard_map/ppermute | solution.py:235
  127.6 93.5 %collective-permute-start.1 = (bf16[16,1024]{1,0:T(8,128)(2,1)S(1)}, bf16[16,1024]{1,0:T(8,128)(2,1)S(1)}, u32[]{:S(2)}, u32[]{:S(2)}) collective-permute-start(bf16[16,1024]{1,0:T(8,128)(2,1)S(1)} %bitcast.87), channel_id=1, source_target_pairs={{0,16},{4,20},{8,24},{12,28},{16,32},{20,36},{24,40},{28,44},{32,4... | collective-permute-start | bytes 98312 | tf_op jit(solution)/shard_map/ppermute | solution.py:235
  129.0 93.8 %collective-permute-start.2 = (bf16[16,1024]{1,0:T(8,128)(2,1)S(1)}, bf16[16,1024]{1,0:T(8,128)(2,1)S(1)}, u32[]{:S(2)}, u32[]{:S(2)}) collective-permute-start(bf16[16,1024]{1,0:T(8,128)(2,1)S(1)} %bitcast.88), channel_id=1, source_target_pairs={{0,24},{4,28},{8,32},{12,36},{16,40},{20,44},{24,48},{28,52},{32,5... | collective-permute-start | bytes 98312 | tf_op jit(solution)/shard_map/ppermute | solution.py:235
  131.4 95.3 %collective-permute-start.3 = (bf16[16,1024]{1,0:T(8,128)(2,1)S(1)}, bf16[16,1024]{1,0:T(8,128)(2,1)S(1)}, u32[]{:S(2)}, u32[]{:S(2)}) collective-permute-start(bf16[16,1024]{1,0:T(8,128)(2,1)S(1)} %bitcast.89), channel_id=1, source_target_pairs={{0,32},{4,36},{8,40},{12,44},{16,48},{20,52},{24,56},{28,60},{32,0... | collective-permute-start | bytes 98312 | tf_op jit(solution)/shard_map/ppermute | solution.py:235
  133.4 93.2 %collective-permute-start.4 = (bf16[16,1024]{1,0:T(8,128)(2,1)S(1)}, bf16[16,1024]{1,0:T(8,128)(2,1)S(1)}, u32[]{:S(2)}, u32[]{:S(2)}) collective-permute-start(bf16[16,1024]{1,0:T(8,128)(2,1)S(1)} %bitcast.90), channel_id=1, source_target_pairs={{0,40},{4,44},{8,48},{12,52},{16,56},{20,60},{24,0},{28,4},{32,8},... | collective-permute-start | bytes 98312 | tf_op jit(solution)/shard_map/ppermute | solution.py:235
  217.1 9.5 %collective-permute-start.5 = (bf16[16,1024]{1,0:T(8,128)(2,1)S(1)}, bf16[16,1024]{1,0:T(8,128)(2,1)S(1)}, u32[]{:S(2)}, u32[]{:S(2)}) collective-permute-start(bf16[16,1024]{1,0:T(8,128)(2,1)S(1)} %bitcast.91), channel_id=1, source_target_pairs={{0,48},{4,52},{8,56},{12,60},{16,0},{20,4},{24,8},{28,12},{32,16},... | collective-permute-start | bytes 98312 | tf_op jit(solution)/shard_map/ppermute | solution.py:235
  221.0 5.6 %collective-permute-start.6 = (bf16[16,1024]{1,0:T(8,128)(2,1)S(1)}, bf16[16,1024]{1,0:T(8,128)(2,1)S(1)}, u32[]{:S(2)}, u32[]{:S(2)}) collective-permute-start(bf16[16,1024]{1,0:T(8,128)(2,1)S(1)} %bitcast.92), channel_id=1, source_target_pairs={{0,56},{4,60},{8,0},{12,4},{16,8},{20,12},{24,16},{28,20},{32,24},... | collective-permute-start | bytes 98312 | tf_op jit(solution)/shard_map/ppermute | solution.py:235
  226.7 9.7 %collective-permute-start.7 = (bf16[8,16,1024]{2,1,0:T(8,128)(2,1)S(1)}, bf16[8,16,1024]{2,1,0:T(8,128)(2,1)S(1)}, u32[]{:S(2)}, u32[]{:S(2)}) collective-permute-start(bf16[8,16,1024]{2,1,0:T(8,128)(2,1)S(1)} %bitcast_dynamic-update-slice_fusion.1), channel_id=1, source_target_pairs={{0,64},{4,68},{8,72},{12,76},{16,80},{20,84},{24,88},{28,92},{32,9... | collective-permute-start | bytes 786440 | tf_op jit(solution)/shard_map/ppermute | solution.py:235
  226.9 12.6 %collective-permute-start.8 = (bf16[8,16,1024]{2,1,0:T(8,128)(2,1)S(1)}, bf16[8,16,1024]{2,1,0:T(8,128)(2,1)S(1)}, u32[]{:S(2)}, u32[]{:S(2)}) collective-permute-start(bf16[8,16,1024]{2,1,0:T(8,128)(2,1)S(1)} %bitcast_dynamic-update-slice_fusion.1), channel_id=1, source_target_pairs={{0,128},{4,132},{8,136},{12,140},{16,144},{20,148},{24,152},{28,15... | collective-permute-start | bytes 786440 | tf_op jit(solution)/shard_map/ppermute | solution.py:235
  229.5 11.9 %collective-permute-start.9 = (bf16[8,16,1024]{2,1,0:T(8,128)(2,1)S(1)}, bf16[8,16,1024]{2,1,0:T(8,128)(2,1)S(1)}, u32[]{:S(2)}, u32[]{:S(2)}) collective-permute-start(bf16[8,16,1024]{2,1,0:T(8,128)(2,1)S(1)} %bitcast_dynamic-update-slice_fusion.1), channel_id=1, source_target_pairs={{0,192},{4,196},{8,200},{12,204},{16,208},{20,212},{24,216},{28,22... | collective-permute-start | bytes 786440 | tf_op jit(solution)/shard_map/ppermute | solution.py:235
  241.6 3.9 %collective-permute-start.10 = (bf16[4,8,16,1024]{3,2,1,0:T(8,128)(2,1)S(1)}, bf16[4,8,16,1024]{3,2,1,0:T(8,128)(2,1)S(1)}, u32[]{:S(2)}, u32[]{:S(2)}) collective-permute-start(bf16[4,8,16,1024]{3,2,1,0:T(8,128)(2,1)S(1)} %get-tuple-element.8), channel_id=1, source_target_pairs={{0,4},{4,0},{8,12},{12,8},{16,20},{20,16},{24,28},{28,24},{32,36},... | collective-permute-start | bytes 3145736 | tf_op jit(solution)/shard_map/ppermute | solution.py:235
  245.5 1.1 copy-start.4
  250.0 9.4 %copy-start.3 = (bf16[64,16,1024]{2,1,0:T(8,128)(2,1)S(1)}, bf16[64,16,1024]{2,1,0:T(8,128)(2,1)}, u32[]{:S(2)}) copy-start(bf16[64,16,1024]{2,1,0:T(8,128)(2,1)} %gather_fusion.3) | copy-start | bytes 6291460
  257.5 2.0 copy-start.2
